TPU v7x, 512 devices: a whole 4x8x8 slice. The times are simulated.
512 devices in a mesh: owner: 64 (over y, x, core), rows: 8 (over z).
Axes of the slice: x: 4, y: 8, z: 8, core: 2. Of those that a mesh axis runs over, the one named last changes fastest.
Arguments:
- train_down: float32 [64, 1024, 2048], P('owner', None, 'rows'), may hold values from -0.1875 to 0.1875
- router_weight: float32 [2048, 64], P('rows', 'owner'), may hold values from -0.125 to 0.125
- router_gain: float32 [2048], P('rows'), may hold values from 0.25 to 1.75
Outputs:
- ready_down: bfloat16 [64, 2048, 1024], P('owner')
- serve_router: bfloat16 [2048, 64], replicated
All inputs are finite; a program needn't handle non-finite values.
Results may differ from a plain program's by a relative error of at most 0.001.
Values may be sent and summed in bfloat16 or wider, within the bound.
No kernel may reach another device: no remote copies, remote signals or barrier semaphores. Data moves between devices by JAX's collectives and lax.ppermute only.
A program may use at most 64 MiB of HBM per device.

v0:
```python
import jax
import jax.numpy as jnp
from jax import lax
from jax.experimental import pallas as pl
from jax.experimental.pallas import tpu as pltpu
from jax.sharding import Mesh
from jax.sharding import PartitionSpec as P


OWNER = ("y", "x", "core")


def a2a(values, axis):
    copies = jnp.broadcast_to(values, (lax.axis_size(axis), *values.shape))
    return lax.all_to_all(copies, axis, split_axis=0, concat_axis=0, tiled=True)


def put(out, arrays, pieces, shape=None):
    count = len(pieces)
    fresh = out is None

    def body(*refs):
        out_ref, sems = refs[-2:]
        n = lax.axis_size("rows")
        rows = out_ref.shape[0] // n
        z, way = lax.axis_index("rows"), 1 - 2 * lax.axis_index("core")
        copies = []
        for i, (which, part, turn) in enumerate(pieces):
            at = pl.multiple_of(((z + turn * way + n) % n) * rows, rows)
            src = refs[which].at[pl.ds(part * rows, rows)]
            copies.append(pltpu.make_async_copy(src, out_ref.at[pl.ds(at, rows)], sems.at[i]))
        for copy in copies:
            copy.start()
        for copy in copies:
            copy.wait()

    arrays = [pltpu.with_memory_space_constraint(a, pltpu.VMEM) for a in arrays]
    whole = pl.BlockSpec(memory_space=pl.ANY)
    return pl.pallas_call(
        body,
        out_shape=jax.ShapeDtypeStruct(shape if fresh else out.shape, jnp.bfloat16),
        in_specs=[pl.BlockSpec(memory_space=pltpu.VMEM)] * len(arrays) + [whole] * (not fresh),
        out_specs=whole,
        scratch_shapes=[pltpu.SemaphoreType.DMA((count,))],
        compiler_params=pltpu.CompilerParams(vmem_limit_bytes=8 << 20),
        input_output_aliases={} if fresh else {len(arrays): 0},
    )(*arrays, *([] if fresh else [out]))


def on_device(train_down, router_weight, router_gain):
    n, g = lax.axis_size("rows"), lax.axis_size(OWNER)
    ax = (*OWNER, "rows")

    def pairs(turn, core):
        out = []
        for a in range(g):
            for i in range(n):
                way = 1 if (a + core) % 2 == 0 else -1
                out.append((a * n + i, (a ^ turn) * n + (i + way) % n))
        return out

    along = pairs(0, 0)
    cross_first = pairs(1, 1)
    cross_last = pairs(1, 0)
    across = [(a * n + i, (a ^ 1) * n + i) for a in range(g) for i in range(n)]

    def send(x, perm):
        return lax.ppermute(x, ax, perm)

    block = jnp.transpose(train_down[0]).astype(jnp.bfloat16)
    rows, width = block.shape

    o1 = send(block, along)
    p1 = send(block, cross_first)
    column = (router_weight[:, 0] * router_gain).astype(jnp.bfloat16).reshape(2, -1)
    column = a2a(column, "rows").reshape(-1, column.shape[1])
    o2 = send(o1, along)
    p2 = send(p1, along)
    table = a2a(column, "y")
    o3 = send(o2, along)
    p3 = send(p2, cross_last)
    table = a2a(table, ("x", "core"))
    table = jnp.swapaxes(table, 0, 1).reshape(g, -1)
    o4 = send(o3, along)
    q1 = send(p1, across)
    q2 = send(p2, across)
    out = put(
        None,
        [block, o1, o2, o3, q1, q2, p3],
        [(0, 0, 0), (1, 0, -1), (2, 0, -2), (3, 0, -3), (4, 0, 1), (5, 0, 2), (6, 0, 3)],
        (n * rows, width),
    )
    out = put(out, [o4], [(0, 0, -4)])
    return (out[None], jnp.transpose(table))


def solution(mesh):
    m = Mesh(mesh.devices.reshape(8, 4, 2, 8), (*OWNER, "rows"))
    in_specs = (P(OWNER, None, "rows"), P("rows", OWNER), P("rows"))
    out_specs = (P(OWNER, None, None), P())
    return jax.shard_map(
        on_device, mesh=m, in_specs=in_specs, out_specs=out_specs, check_vma=False
    )
```

profile of v0, /device:TPU:1, one launch (start us, length us, event | category | flops | bytes accessed | tf_op | source)
XLA Modules:
  0.0 84.8 jit_solution(8835476418932221966)
XLA Ops:
  0.6 1.4 %copy.8 = bf16[1,1024,256]{1,2,0:T(8,128)(2,1)S(1)} copy(f32[1,1024,256]{2,1,0:T(8,128)} %param.3) | data formatting | bytes 1572864 | tf_op args[0]
  2.1 11.5 %collective-permute-start = (bf16[256,1024]{1,0:T(8,128)(2,1)S(1)}, bf16[256,1024]{1,0:T(8,128)(2,1)S(1)}, u32[]{:S(2)}, u32[]{:S(2)}) collective-permute-start(bf16[256,1024]{1,0:T(8,128)(2,1)S(1)} %bitcast.22), channel_id=1, source_target_pairs={{0,1},{1,2},{2,3},{3,4},{4,5},{5,6},{6,7},{7,0},{8,15},{9,8},{10,9... | collective-permute-start | bytes 1572872 | tf_op jit(solution)/shard_map/ppermute | solution.py:68
  13.6 1.9 %collective-permute-start.4 = (bf16[256,1024]{1,0:T(8,128)(2,1)S(1)}, bf16[256,1024]{1,0:T(8,128)(2,1)}, u32[]{:S(2)}, u32[]{:S(2)}) collective-permute-start(bf16[256,1024]{1,0:T(8,128)(2,1)S(1)} %bitcast.23), channel_id=1, source_target_pairs={{0,15},{1,8},{2,9},{3,10},{4,11},{5,12},{6,13},{7,14},{8,1},{9,2},... | collective-permute-start | bytes 1572872 | tf_op jit(solution)/shard_map/ppermute | solution.py:68
  15.5 7.0 %collective-permute-done.refs_1_ = bf16[256,1024]{1,0:T(8,128)(2,1)S(1)} collective-permute-done((bf16[256,1024]{1,0:T(8,128)(2,1)S(1)}, bf16[256,1024]{1,0:T(8,128)(2,1)S(1)}, u32[]{:S(2)}, u32[]{:S(2)}) %collective-permute-start) | collective-permute-done | bytes 524320 | tf_op jit(solution)/shard_map/ppermute | solution.py:68
  22.5 5.0 %collective-permute-start.1 = (bf16[256,1024]{1,0:T(8,128)(2,1)S(1)}, bf16[256,1024]{1,0:T(8,128)(2,1)S(1)}, u32[]{:S(2)}, u32[]{:S(2)}) collective-permute-start(bf16[256,1024]{1,0:T(8,128)(2,1)S(1)} %collective-permute-done.refs_1_), channel_id=1, source_target_pairs={{0,1},{1,2},{2,3},{3,4},{4,5},{5,6},{6,7},{7,0},{8,15},{9,8},{10,9... | collective-permute-start | bytes 1572872 | tf_op jit(solution)/shard_map/ppermute | solution.py:68
  27.5 0.0 collective-permute-done.4
  27.5 2.9 %collective-permute-start.6 = (bf16[256,1024]{1,0:T(8,128)(2,1)}, bf16[256,1024]{1,0:T(8,128)(2,1)}, u32[]{:S(2)}, u32[]{:S(2)}) collective-permute-start(bf16[256,1024]{1,0:T(8,128)(2,1)} %collective-permute-done.4), channel_id=1, source_target_pairs={{0,1},{1,2},{2,3},{3,4},{4,5},{5,6},{6,7},{7,0},{8,15},{9,8},{10,9... | collective-permute-start | bytes 1572872 | tf_op jit(solution)/shard_map/ppermute | solution.py:68
  30.4 3.2 %collective-permute-done.1.refs_2_ = bf16[256,1024]{1,0:T(8,128)(2,1)S(1)} collective-permute-done((bf16[256,1024]{1,0:T(8,128)(2,1)S(1)}, bf16[256,1024]{1,0:T(8,128)(2,1)S(1)}, u32[]{:S(2)}, u32[]{:S(2)}) %collective-permute-start.1) | collective-permute-done | bytes 524320 | tf_op jit(solution)/shard_map/ppermute | solution.py:68
  33.6 5.0 %collective-permute-start.2 = (bf16[256,1024]{1,0:T(8,128)(2,1)S(1)}, bf16[256,1024]{1,0:T(8,128)(2,1)S(1)}, u32[]{:S(2)}, u32[]{:S(2)}) collective-permute-start(bf16[256,1024]{1,0:T(8,128)(2,1)S(1)} %collective-permute-done.1.refs_2_), channel_id=1, source_target_pairs={{0,1},{1,2},{2,3},{3,4},{4,5},{5,6},{6,7},{7,0},{8,15},{9,8},{10,9... | collective-permute-start | bytes 1572872 | tf_op jit(solution)/shard_map/ppermute | solution.py:68
  38.7 0.7 fusion
  39.4 8.9 %all_to_all.15 = bf16[8,2,128]{2,1,0:T(2,128)(2,1)S(1)} all-to-all(bf16[8,2,128]{2,1,0:T(2,128)(2,1)S(1)} %broadcast_in_dim.13), channel_id=1, replica_groups=mesh['y'=8,'x'=4,'core'=2,'rows'=8] {'rows'}, dimensions={0} | all-to-all | bytes 8192 | tf_op jit(solution)/shard_map/all_to_all | solution.py:15
  48.3 0.6 broadcast_in_dim.14
  48.9 6.8 %all-to-all-start.1 = ((bf16[8,16,128]{2,1,0:T(8,128)(2,1)}), bf16[8,16,128]{2,1,0:T(8,128)(2,1)S(1)}, u32[]{:S(2)}, u32[]{:S(2)}) async-start(bf16[8,16,128]{2,1,0:T(8,128)(2,1)} %broadcast_in_dim.14), calls=%async_computation.1 | async-start | bytes 65536 | tf_op jit(solution)/shard_map/all_to_all | solution.py:15
  55.7 6.7 %collective-permute-start.5 = (bf16[256,1024]{1,0:T(8,128)(2,1)}, bf16[256,1024]{1,0:T(8,128)(2,1)S(1)}, u32[]{:S(2)}, u32[]{:S(2)}) collective-permute-start(bf16[256,1024]{1,0:T(8,128)(2,1)} %collective-permute-done.4), channel_id=1, source_target_pairs={{0,8},{1,9},{2,10},{3,11},{4,12},{5,13},{6,14},{7,15},{8,0},{9,1},... | collective-permute-start | bytes 1572872 | tf_op jit(solution)/shard_map/ppermute | solution.py:68
  62.5 0.0 collective-permute-done.6
  62.5 1.9 %collective-permute-start.7 = (bf16[256,1024]{1,0:T(8,128)(2,1)}, bf16[256,1024]{1,0:T(8,128)(2,1)}, u32[]{:S(2)}, u32[]{:S(2)}) collective-permute-start(bf16[256,1024]{1,0:T(8,128)(2,1)} %collective-permute-done.6), channel_id=1, source_target_pairs={{0,8},{1,9},{2,10},{3,11},{4,12},{5,13},{6,14},{7,15},{8,0},{9,1},... | collective-permute-start | bytes 1572872 | tf_op jit(solution)/shard_map/ppermute | solution.py:68
  64.4 2.6 %collective-permute-start.8 = (bf16[256,1024]{1,0:T(8,128)(2,1)}, bf16[256,1024]{1,0:T(8,128)(2,1)}, u32[]{:S(2)}, u32[]{:S(2)}) collective-permute-start(bf16[256,1024]{1,0:T(8,128)(2,1)} %collective-permute-done.6), channel_id=1, source_target_pairs={{0,9},{1,10},{2,11},{3,12},{4,13},{5,14},{6,15},{7,8},{8,7},{9,0},... | collective-permute-start | bytes 1572872 | tf_op jit(solution)/shard_map/ppermute | solution.py:68
  67.0 0.0 collective-permute-done.2.refs_3_
  67.0 2.2 %collective-permute-start.3 = (bf16[256,1024]{1,0:T(8,128)(2,1)S(1)}, bf16[256,1024]{1,0:T(8,128)(2,1)S(1)}, u32[]{:S(2)}, u32[]{:S(2)}) collective-permute-start(bf16[256,1024]{1,0:T(8,128)(2,1)S(1)} %collective-permute-done.2.refs_3_), channel_id=1, source_target_pairs={{0,1},{1,2},{2,3},{3,4},{4,5},{5,6},{6,7},{7,0},{8,15},{9,8},{10,9... | collective-permute-start | bytes 1572872 | tf_op jit(solution)/shard_map/ppermute | solution.py:68
  69.2 0.0 all-to-all-done.1
  69.3 10.8 %all_to_all.16 = bf16[8,8,16,128]{3,2,1,0:T(8,128)(2,1)S(1)} all-to-all(bf16[8,8,16,128]{3,2,1,0:T(8,128)(2,1)S(1)} %broadcast_in_dim.15), channel_id=1, replica_groups=mesh['y'=8,'x'=4,'core'=2,'rows'=8] {'x','core'}, dimensions={0} | all-to-all | bytes 524288 | tf_op jit(solution)/shard_map/all_to_all | solution.py:15
  80.1 0.8 copy.13
  80.9 0.0 collective-permute-done.5.refs_4_
  80.9 0.0 collective-permute-done.7.refs_5_
  80.9 0.0 collective-permute-done.8.refs_6_
  80.9 3.1 %shard_map.50.refs_1_ = bf16[2048,1024]{1,0:T(8,128)(2,1)} custom-call(bf16[256,1024]{1,0:T(8,128)(2,1)S(1)} %bitcast.24, bf16[256,1024]{1,0:T(8,128)(2,1)S(1)} %collective-permute-done.refs_1_, bf16[256,1024]{1,0:T(8,128)(2,1)S(1)} %collective-permute-done.1.refs_2_, bf16[256,1024]{1,0:T(8,128)(2,1)S(1)} %collective-permute-done.2.refs_3_, ...), custom_call_target="tpu_custom_call" | custom-call | tf_op jit(solution)/shard_map/pallas_call | solution.py:39
  84.0 0.0 collective-permute-done.3.refs_0_
  84.0 0.8 shard_map.51
  (3 shorter events, 0.1 us)
Async XLA Ops:
  2.1 20.4 %collective-permute-start = (bf16[256,1024]{1,0:T(8,128)(2,1)S(1)}, bf16[256,1024]{1,0:T(8,128)(2,1)S(1)}, u32[]{:S(2)}, u32[]{:S(2)}) collective-permute-start(bf16[256,1024]{1,0:T(8,128)(2,1)S(1)} %bitcast.22), channel_id=1, source_target_pairs={{0,1},{1,2},{2,3},{3,4},{4,5},{5,6},{6,7},{7,0},{8,15},{9,8},{10,9... | collective-permute-start | bytes 1572872 | tf_op jit(solution)/shard_map/ppermute | solution.py:68
  13.6 14.0 %collective-permute-start.4 = (bf16[256,1024]{1,0:T(8,128)(2,1)S(1)}, bf16[256,1024]{1,0:T(8,128)(2,1)}, u32[]{:S(2)}, u32[]{:S(2)}) collective-permute-start(bf16[256,1024]{1,0:T(8,128)(2,1)S(1)} %bitcast.23), channel_id=1, source_target_pairs={{0,15},{1,8},{2,9},{3,10},{4,11},{5,12},{6,13},{7,14},{8,1},{9,2},... | collective-permute-start | bytes 1572872 | tf_op jit(solution)/shard_map/ppermute | solution.py:68
  22.5 11.1 %collective-permute-start.1 = (bf16[256,1024]{1,0:T(8,128)(2,1)S(1)}, bf16[256,1024]{1,0:T(8,128)(2,1)S(1)}, u32[]{:S(2)}, u32[]{:S(2)}) collective-permute-start(bf16[256,1024]{1,0:T(8,128)(2,1)S(1)} %collective-permute-done.refs_1_), channel_id=1, source_target_pairs={{0,1},{1,2},{2,3},{3,4},{4,5},{5,6},{6,7},{7,0},{8,15},{9,8},{10,9... | collective-permute-start | bytes 1572872 | tf_op jit(solution)/shard_map/ppermute | solution.py:68
  27.5 34.9 %collective-permute-start.6 = (bf16[256,1024]{1,0:T(8,128)(2,1)}, bf16[256,1024]{1,0:T(8,128)(2,1)}, u32[]{:S(2)}, u32[]{:S(2)}) collective-permute-start(bf16[256,1024]{1,0:T(8,128)(2,1)} %collective-permute-done.4), channel_id=1, source_target_pairs={{0,1},{1,2},{2,3},{3,4},{4,5},{5,6},{6,7},{7,0},{8,15},{9,8},{10,9... | collective-permute-start | bytes 1572872 | tf_op jit(solution)/shard_map/ppermute | solution.py:68
  33.6 33.3 %collective-permute-start.2 = (bf16[256,1024]{1,0:T(8,128)(2,1)S(1)}, bf16[256,1024]{1,0:T(8,128)(2,1)S(1)}, u32[]{:S(2)}, u32[]{:S(2)}) collective-permute-start(bf16[256,1024]{1,0:T(8,128)(2,1)S(1)} %collective-permute-done.1.refs_2_), channel_id=1, source_target_pairs={{0,1},{1,2},{2,3},{3,4},{4,5},{5,6},{6,7},{7,0},{8,15},{9,8},{10,9... | collective-permute-start | bytes 1572872 | tf_op jit(solution)/shard_map/ppermute | solution.py:68
  48.9 20.3 %all-to-all-start.1 = ((bf16[8,16,128]{2,1,0:T(8,128)(2,1)}), bf16[8,16,128]{2,1,0:T(8,128)(2,1)S(1)}, u32[]{:S(2)}, u32[]{:S(2)}) async-start(bf16[8,16,128]{2,1,0:T(8,128)(2,1)} %broadcast_in_dim.14), calls=%async_computation.1 | async-start | bytes 65536 | tf_op jit(solution)/shard_map/all_to_all | solution.py:15
  55.7 25.2 %collective-permute-start.5 = (bf16[256,1024]{1,0:T(8,128)(2,1)}, bf16[256,1024]{1,0:T(8,128)(2,1)S(1)}, u32[]{:S(2)}, u32[]{:S(2)}) collective-permute-start(bf16[256,1024]{1,0:T(8,128)(2,1)} %collective-permute-done.4), channel_id=1, source_target_pairs={{0,8},{1,9},{2,10},{3,11},{4,12},{5,13},{6,14},{7,15},{8,0},{9,1},... | collective-permute-start | bytes 1572872 | tf_op jit(solution)/shard_map/ppermute | solution.py:68
  62.5 18.4 %collective-permute-start.7 = (bf16[256,1024]{1,0:T(8,128)(2,1)}, bf16[256,1024]{1,0:T(8,128)(2,1)}, u32[]{:S(2)}, u32[]{:S(2)}) collective-permute-start(bf16[256,1024]{1,0:T(8,128)(2,1)} %collective-permute-done.6), channel_id=1, source_target_pairs={{0,8},{1,9},{2,10},{3,11},{4,12},{5,13},{6,14},{7,15},{8,0},{9,1},... | collective-permute-start | bytes 1572872 | tf_op jit(solution)/shard_map/ppermute | solution.py:68
  64.4 16.5 %collective-permute-start.8 = (bf16[256,1024]{1,0:T(8,128)(2,1)}, bf16[256,1024]{1,0:T(8,128)(2,1)}, u32[]{:S(2)}, u32[]{:S(2)}) collective-permute-start(bf16[256,1024]{1,0:T(8,128)(2,1)} %collective-permute-done.6), channel_id=1, source_target_pairs={{0,9},{1,10},{2,11},{3,12},{4,13},{5,14},{6,15},{7,8},{8,7},{9,0},... | collective-permute-start | bytes 1572872 | tf_op jit(solution)/shard_map/ppermute | solution.py:68
  67.0 17.0 %collective-permute-start.3 = (bf16[256,1024]{1,0:T(8,128)(2,1)S(1)}, bf16[256,1024]{1,0:T(8,128)(2,1)S(1)}, u32[]{:S(2)}, u32[]{:S(2)}) collective-permute-start(bf16[256,1024]{1,0:T(8,128)(2,1)S(1)} %collective-permute-done.2.refs_3_), channel_id=1, source_target_pairs={{0,1},{1,2},{2,3},{3,4},{4,5},{5,6},{6,7},{7,0},{8,15},{9,8},{10,9... | collective-permute-start | bytes 1572872 | tf_op jit(solution)/shard_map/ppermute | solution.py:68
where the time goes:
time: 85.4 us; the launch traced here: 84.8 us
  starting transfers between devices  46.5 us (54%)
  blocking collectives  19.8 us (23%)
  waiting for transfers between devices  10.3 us (12%)
  Pallas kernels  3.91 us (5%)
  local copies, waits for them, and re-layouts  2.88 us (3%)
    ppermute x9, starting transfers between devices, send(): return lax.ppermute(x, ax, perm)  39.7 us
    all_to_all x2, blocking collectives, a2a(): return lax.all_to_all(copies, axis, split_axis=0, concat_axis=0, tiled=True)  19.8 us
    ppermute x9, waiting for transfers between devices, send(): return lax.ppermute(x, ax, perm)  10.3 us
    all_to_all x1, starting transfers between devices, a2a(): return lax.all_to_all(copies, axis, split_axis=0, concat_axis=0, tiled=True)  6.82 us
    pallas_call x2, Pallas kernels, put(): pl.pallas_call(body, out_shape=jax.ShapeDtypeStruct(shape if fresh else o...  3.91 us
    unnamed x3, local copies, waits for them, and re-layouts  2.22 us
  transfers between devices with their start and end apart: 10, of which 2 were waited for; matrix products, arithmetic and copies ran while one was open for 3% of the time, Pallas kernels for 4%

commit v1 on v0

--- a/solution.py
+++ b/solution.py
@@ -71,26 +71,25 @@
     rows, width = block.shape
 
     o1 = send(block, along)
+    out = put(None, [block], [(0, 0, 0)], (n * rows, width))
     p1 = send(block, cross_first)
     column = (router_weight[:, 0] * router_gain).astype(jnp.bfloat16).reshape(2, -1)
-    column = a2a(column, "rows").reshape(-1, column.shape[1])
+    table = a2a(column, "y")
     o2 = send(o1, along)
     p2 = send(p1, along)
-    table = a2a(column, "y")
+    table = a2a(table, "rows")
+    table = jnp.swapaxes(table, 0, 1).reshape(-1, 2 * n, column.shape[1])
     o3 = send(o2, along)
     p3 = send(p2, cross_last)
     table = a2a(table, ("x", "core"))
-    table = jnp.swapaxes(table, 0, 1).reshape(g, -1)
     o4 = send(o3, along)
     q1 = send(p1, across)
     q2 = send(p2, across)
-    out = put(
-        None,
-        [block, o1, o2, o3, q1, q2, p3],
-        [(0, 0, 0), (1, 0, -1), (2, 0, -2), (3, 0, -3), (4, 0, 1), (5, 0, 2), (6, 0, 3)],
-        (n * rows, width),
-    )
+    out = put(out, [o1, o2, o3, p3], [(0, 0, -1), (1, 0, -2), (2, 0, -3), (3, 0, 3)])
+    table, out = lax.optimization_barrier((table, out))
+    out = put(out, [q1, q2], [(0, 0, 1), (1, 0, 2)])
     out = put(out, [o4], [(0, 0, -4)])
+    table = jnp.swapaxes(table, 0, 1).reshape(g, -1)
     return (out[None], jnp.transpose(table))
 
 

time: 85.4 us -> 89.8 us (1.052)
  blocking collectives: 19.8 us -> 13.2 us
  starting transfers between devices: 46.5 us -> 50.6 us
  waiting for transfers between devices: 10.3 us -> 14.2 us
  Pallas kernels: 3.91 us -> 6.02 us
    all_to_all x2 -> x1, blocking collectives: 19.8 us -> 13.2 us  [a2a(): return lax.all_to_all(copies, axis, split_axis=0, concat_axis=0, tiled=True)]
    all_to_all x1 -> x2, waiting for transfers between devices: 0.01 us -> 3.26 us  [a2a(): return lax.all_to_all(copies, axis, split_axis=0, concat_axis=0, tiled=True)]
    ppermute x9, starting transfers between devices: 39.7 us -> 42.8 us  [send(): return lax.ppermute(x, ax, perm)]
    pallas_call x2 -> x4, Pallas kernels: 3.91 us -> 6.02 us  [put(): pl.pallas_call(body, out_shape=jax.ShapeDtypeStruct(shape if fresh else o...]
    all_to_all x1 -> x2, starting transfers between devices: 6.82 us -> 7.75 us  [a2a(): return lax.all_to_all(copies, axis, split_axis=0, concat_axis=0, tiled=True)]
  transfers between devices with their start and end apart: 10 -> 11, of which waited for: 2 -> 4; matrix products, arithmetic and copies ran while one was open for 3% -> 3% of each run, Pallas kernels for 4% -> 5%
where the time goes in v1:
time: 89.8 us; the launch traced here: 89.1 us
  starting transfers between devices  50.6 us (56%)
  waiting for transfers between devices  14.2 us (16%)
  blocking collectives  13.2 us (15%)
  Pallas kernels  6.02 us (7%)
  local copies, waits for them, and re-layouts  3.61 us (4%)
    ppermute x9, starting transfers between devices, send(): return lax.ppermute(x, ax, perm)  42.8 us
    all_to_all x1, blocking collectives, a2a(): return lax.all_to_all(copies, axis, split_axis=0, concat_axis=0, tiled=True)  13.2 us
    ppermute x9, waiting for transfers between devices, send(): return lax.ppermute(x, ax, perm)  11 us
    all_to_all x2, starting transfers between devices, a2a(): return lax.all_to_all(copies, axis, split_axis=0, concat_axis=0, tiled=True)  7.75 us
    pallas_call x4, Pallas kernels, put(): pl.pallas_call(body, out_shape=jax.ShapeDtypeStruct(shape if fresh else o...  6.02 us
    all_to_all x2, waiting for transfers between devices, a2a(): return lax.all_to_all(copies, axis, split_axis=0, concat_axis=0, tiled=True)  3.26 us
    unnamed x3, local copies, waits for them, and re-layouts  2.22 us
  transfers between devices with their start and end apart: 11, of which 4 were waited for; matrix products, arithmetic and copies ran while one was open for 3% of the time, Pallas kernels for 5%

profile of v1, /device:TPU:1, one launch (start us, length us, event | category | flops | bytes accessed | tf_op | source)
XLA Modules:
  0.0 89.1 jit_solution(4463865874564654012)
XLA Ops:
  0.6 1.4 %copy.10 = bf16[1,1024,256]{1,2,0:T(8,128)(2,1)S(1)} copy(f32[1,1024,256]{2,1,0:T(8,128)} %param.3) | data formatting | bytes 1572864 | tf_op args[0]
  2.1 11.5 %collective-permute-start = (bf16[256,1024]{1,0:T(8,128)(2,1)S(1)}, bf16[256,1024]{1,0:T(8,128)(2,1)S(1)}, u32[]{:S(2)}, u32[]{:S(2)}) collective-permute-start(bf16[256,1024]{1,0:T(8,128)(2,1)S(1)} %bitcast.24), channel_id=1, source_target_pairs={{0,1},{1,2},{2,3},{3,4},{4,5},{5,6},{6,7},{7,0},{8,15},{9,8},{10,9... | collective-permute-start | bytes 1572872 | tf_op jit(solution)/shard_map/ppermute | solution.py:68
  13.6 1.9 %collective-permute-start.4 = (bf16[256,1024]{1,0:T(8,128)(2,1)S(1)}, bf16[256,1024]{1,0:T(8,128)(2,1)}, u32[]{:S(2)}, u32[]{:S(2)}) collective-permute-start(bf16[256,1024]{1,0:T(8,128)(2,1)S(1)} %bitcast.25), channel_id=1, source_target_pairs={{0,15},{1,8},{2,9},{3,10},{4,11},{5,12},{6,13},{7,14},{8,1},{9,2},... | collective-permute-start | bytes 1572872 | tf_op jit(solution)/shard_map/ppermute | solution.py:68
  15.5 7.0 %collective-permute-done.refs_0_ = bf16[256,1024]{1,0:T(8,128)(2,1)S(1)} collective-permute-done((bf16[256,1024]{1,0:T(8,128)(2,1)S(1)}, bf16[256,1024]{1,0:T(8,128)(2,1)S(1)}, u32[]{:S(2)}, u32[]{:S(2)}) %collective-permute-start) | collective-permute-done | bytes 524320 | tf_op jit(solution)/shard_map/ppermute | solution.py:68
  22.5 5.0 %collective-permute-start.1 = (bf16[256,1024]{1,0:T(8,128)(2,1)S(1)}, bf16[256,1024]{1,0:T(8,128)(2,1)S(1)}, u32[]{:S(2)}, u32[]{:S(2)}) collective-permute-start(bf16[256,1024]{1,0:T(8,128)(2,1)S(1)} %collective-permute-done.refs_0_), channel_id=1, source_target_pairs={{0,1},{1,2},{2,3},{3,4},{4,5},{5,6},{6,7},{7,0},{8,15},{9,8},{10,9... | collective-permute-start | bytes 1572872 | tf_op jit(solution)/shard_map/ppermute | solution.py:68
  27.5 0.0 collective-permute-done.4
  27.5 2.9 %collective-permute-start.6 = (bf16[256,1024]{1,0:T(8,128)(2,1)}, bf16[256,1024]{1,0:T(8,128)(2,1)}, u32[]{:S(2)}, u32[]{:S(2)}) collective-permute-start(bf16[256,1024]{1,0:T(8,128)(2,1)} %collective-permute-done.4), channel_id=1, source_target_pairs={{0,1},{1,2},{2,3},{3,4},{4,5},{5,6},{6,7},{7,0},{8,15},{9,8},{10,9... | collective-permute-start | bytes 1572872 | tf_op jit(solution)/shard_map/ppermute | solution.py:68
  30.4 3.2 %collective-permute-done.1.refs_1_ = bf16[256,1024]{1,0:T(8,128)(2,1)S(1)} collective-permute-done((bf16[256,1024]{1,0:T(8,128)(2,1)S(1)}, bf16[256,1024]{1,0:T(8,128)(2,1)S(1)}, u32[]{:S(2)}, u32[]{:S(2)}) %collective-permute-start.1) | collective-permute-done | bytes 524320 | tf_op jit(solution)/shard_map/ppermute | solution.py:68
  33.6 5.0 %collective-permute-start.2 = (bf16[256,1024]{1,0:T(8,128)(2,1)S(1)}, bf16[256,1024]{1,0:T(8,128)(2,1)S(1)}, u32[]{:S(2)}, u32[]{:S(2)}) collective-permute-start(bf16[256,1024]{1,0:T(8,128)(2,1)S(1)} %collective-permute-done.1.refs_1_), channel_id=1, source_target_pairs={{0,1},{1,2},{2,3},{3,4},{4,5},{5,6},{6,7},{7,0},{8,15},{9,8},{10,9... | collective-permute-start | bytes 1572872 | tf_op jit(solution)/shard_map/ppermute | solution.py:68
  38.7 0.7 collective-permute-done.6
  39.4 6.9 %collective-permute-start.8 = (bf16[256,1024]{1,0:T(8,128)(2,1)}, bf16[256,1024]{1,0:T(8,128)(2,1)}, u32[]{:S(2)}, u32[]{:S(2)}) collective-permute-start(bf16[256,1024]{1,0:T(8,128)(2,1)} %collective-permute-done.6), channel_id=1, source_target_pairs={{0,9},{1,10},{2,11},{3,12},{4,13},{5,14},{6,15},{7,8},{8,7},{9,0},... | collective-permute-start | bytes 1572872 | tf_op jit(solution)/shard_map/ppermute | solution.py:68
  46.2 0.7 fusion
  46.9 13.2 %all_to_all.15 = bf16[8,2,128]{2,1,0:T(2,128)(2,1)S(1)} all-to-all(bf16[8,2,128]{2,1,0:T(2,128)(2,1)S(1)} %broadcast_in_dim.12), channel_id=1, replica_groups=mesh['y'=8,'x'=4,'core'=2,'rows'=8] {'y'}, dimensions={0} | all-to-all | bytes 8192 | tf_op jit(solution)/shard_map/all_to_all | solution.py:15
  60.1 0.6 broadcast_in_dim.13
  60.7 3.3 %all-to-all-start.1 = ((bf16[8,8,2,128]{3,2,1,0:T(2,128)(2,1)}), bf16[8,8,2,128]{3,2,1,0:T(2,128)(2,1)S(1)}, u32[]{:S(2)}, u32[]{:S(2)}) async-start(bf16[8,8,2,128]{3,2,1,0:T(2,128)(2,1)} %broadcast_in_dim.13), calls=%async_computation.1 | async-start | bytes 65536 | tf_op jit(solution)/shard_map/all_to_all | solution.py:15
  64.1 3.0 %collective-permute-start.5 = (bf16[256,1024]{1,0:T(8,128)(2,1)}, bf16[256,1024]{1,0:T(8,128)(2,1)S(1)}, u32[]{:S(2)}, u32[]{:S(2)}) collective-permute-start(bf16[256,1024]{1,0:T(8,128)(2,1)} %collective-permute-done.4), channel_id=1, source_target_pairs={{0,8},{1,9},{2,10},{3,11},{4,12},{5,13},{6,14},{7,15},{8,0},{9,1},... | collective-permute-start | bytes 1572872 | tf_op jit(solution)/shard_map/ppermute | solution.py:68
  67.1 1.9 %collective-permute-start.7 = (bf16[256,1024]{1,0:T(8,128)(2,1)}, bf16[256,1024]{1,0:T(8,128)(2,1)S(1)}, u32[]{:S(2)}, u32[]{:S(2)}) collective-permute-start(bf16[256,1024]{1,0:T(8,128)(2,1)} %collective-permute-done.6), channel_id=1, source_target_pairs={{0,8},{1,9},{2,10},{3,11},{4,12},{5,13},{6,14},{7,15},{8,0},{9,1},... | collective-permute-start | bytes 1572872 | tf_op jit(solution)/shard_map/ppermute | solution.py:68
  69.0 0.0 collective-permute-done.2.refs_2_
  69.0 4.8 %collective-permute-start.3 = (bf16[256,1024]{1,0:T(8,128)(2,1)S(1)}, bf16[256,1024]{1,0:T(8,128)(2,1)}, u32[]{:S(2)}, u32[]{:S(2)}) collective-permute-start(bf16[256,1024]{1,0:T(8,128)(2,1)S(1)} %collective-permute-done.2.refs_2_), channel_id=1, source_target_pairs={{0,1},{1,2},{2,3},{3,4},{4,5},{5,6},{6,7},{7,0},{8,15},{9,8},{10,9... | collective-permute-start | bytes 1572872 | tf_op jit(solution)/shard_map/ppermute | solution.py:68
  73.8 0.0 all-to-all-done.1
  73.8 0.7 broadcast_in_dim.14
  74.6 4.4 %all-to-all-start.2 = ((bf16[8,8,16,128]{3,2,1,0:T(8,128)(2,1)}), bf16[8,8,16,128]{3,2,1,0:T(8,128)(2,1)S(1)}, u32[]{:S(2)}, u32[]{:S(2)}) async-start(bf16[8,8,16,128]{3,2,1,0:T(8,128)(2,1)} %broadcast_in_dim.14), calls=%async_computation.2 | async-start | bytes 524288 | tf_op jit(solution)/shard_map/all_to_all | solution.py:15
  79.0 0.8 shard_map.50.refs_4_
  79.8 0.0 collective-permute-done.8.refs_3_
  79.8 2.4 %shard_map.51.refs_2_ = bf16[2048,1024]{1,0:T(8,128)(2,1)} custom-call(bf16[256,1024]{1,0:T(8,128)(2,1)S(1)} %collective-permute-done.refs_0_, bf16[256,1024]{1,0:T(8,128)(2,1)S(1)} %collective-permute-done.1.refs_1_, bf16[256,1024]{1,0:T(8,128)(2,1)S(1)} %collective-permute-done.2.refs_2_, ...), custom_call_target="tpu_custom_call", output_to_operand_aliasing={{}: (4, {})} | custom-call | tf_op jit(solution)/shard_map/pallas_call | solution.py:39
  82.2 3.3 %all-to-all-done.2 = bf16[8,8,16,128]{3,2,1,0:T(8,128)(2,1)S(1)} async-done(((bf16[8,8,16,128]{3,2,1,0:T(8,128)(2,1)}), bf16[8,8,16,128]{3,2,1,0:T(8,128)(2,1)S(1)}, u32[]{:S(2)}, u32[]{:S(2)}) %all-to-all-start.2) | async-done | bytes 262176 | tf_op jit(solution)/shard_map/all_to_all | solution.py:15
  85.5 0.8 copy.17
  86.3 0.0 collective-permute-done.5.refs_0_
  86.3 0.0 collective-permute-done.7.refs_1_
  86.3 1.0 %shard_map.52.refs_1_ = bf16[2048,1024]{1,0:T(8,128)(2,1)} custom-call(bf16[256,1024]{1,0:T(8,128)(2,1)S(1)} %collective-permute-done.5.refs_0_, bf16[256,1024]{1,0:T(8,128)(2,1)S(1)} %collective-permute-done.7.refs_1_, bf16[2048,1024]{1,0:T(8,128)(2,1)} %shard_map.51.refs_2_), custom_call_target="tpu_custom_call", output_to_operand_aliasing={{}: (2, {})} | custom-call | tf_op jit(solution)/shard_map/pallas_call | solution.py:39
  87.3 0.0 collective-permute-done.3.refs_0_
  87.3 1.8 %shard_map.53 = bf16[2048,1024]{1,0:T(8,128)(2,1)} custom-call(bf16[256,1024]{1,0:T(8,128)(2,1)} %collective-permute-done.3.refs_0_, bf16[2048,1024]{1,0:T(8,128)(2,1)} %shard_map.52.refs_1_), custom_call_target="tpu_custom_call", output_to_operand_aliasing={{}: (1, {})} | custom-call | tf_op jit(solution)/shard_map/pallas_call | solution.py:39
  (4 shorter events, 0.0 us)
Async XLA Ops:
  2.1 20.4 %collective-permute-start = (bf16[256,1024]{1,0:T(8,128)(2,1)S(1)}, bf16[256,1024]{1,0:T(8,128)(2,1)S(1)}, u32[]{:S(2)}, u32[]{:S(2)}) collective-permute-start(bf16[256,1024]{1,0:T(8,128)(2,1)S(1)} %bitcast.24), channel_id=1, source_target_pairs={{0,1},{1,2},{2,3},{3,4},{4,5},{5,6},{6,7},{7,0},{8,15},{9,8},{10,9... | collective-permute-start | bytes 1572872 | tf_op jit(solution)/shard_map/ppermute | solution.py:68
  13.6 14.0 %collective-permute-start.4 = (bf16[256,1024]{1,0:T(8,128)(2,1)S(1)}, bf16[256,1024]{1,0:T(8,128)(2,1)}, u32[]{:S(2)}, u32[]{:S(2)}) collective-permute-start(bf16[256,1024]{1,0:T(8,128)(2,1)S(1)} %bitcast.25), channel_id=1, source_target_pairs={{0,15},{1,8},{2,9},{3,10},{4,11},{5,12},{6,13},{7,14},{8,1},{9,2},... | collective-permute-start | bytes 1572872 | tf_op jit(solution)/shard_map/ppermute | solution.py:68
  22.5 11.1 %collective-permute-start.1 = (bf16[256,1024]{1,0:T(8,128)(2,1)S(1)}, bf16[256,1024]{1,0:T(8,128)(2,1)S(1)}, u32[]{:S(2)}, u32[]{:S(2)}) collective-permute-start(bf16[256,1024]{1,0:T(8,128)(2,1)S(1)} %collective-permute-done.refs_0_), channel_id=1, source_target_pairs={{0,1},{1,2},{2,3},{3,4},{4,5},{5,6},{6,7},{7,0},{8,15},{9,8},{10,9... | collective-permute-start | bytes 1572872 | tf_op jit(solution)/shard_map/ppermute | solution.py:68
  27.5 11.8 %collective-permute-start.6 = (bf16[256,1024]{1,0:T(8,128)(2,1)}, bf16[256,1024]{1,0:T(8,128)(2,1)}, u32[]{:S(2)}, u32[]{:S(2)}) collective-permute-start(bf16[256,1024]{1,0:T(8,128)(2,1)} %collective-permute-done.4), channel_id=1, source_target_pairs={{0,1},{1,2},{2,3},{3,4},{4,5},{5,6},{6,7},{7,0},{8,15},{9,8},{10,9... | collective-permute-start | bytes 1572872 | tf_op jit(solution)/shard_map/ppermute | solution.py:68
  33.6 35.4 %collective-permute-start.2 = (bf16[256,1024]{1,0:T(8,128)(2,1)S(1)}, bf16[256,1024]{1,0:T(8,128)(2,1)S(1)}, u32[]{:S(2)}, u32[]{:S(2)}) collective-permute-start(bf16[256,1024]{1,0:T(8,128)(2,1)S(1)} %collective-permute-done.1.refs_1_), channel_id=1, source_target_pairs={{0,1},{1,2},{2,3},{3,4},{4,5},{5,6},{6,7},{7,0},{8,15},{9,8},{10,9... | collective-permute-start | bytes 1572872 | tf_op jit(solution)/shard_map/ppermute | solution.py:68
  39.4 40.4 %collective-permute-start.8 = (bf16[256,1024]{1,0:T(8,128)(2,1)}, bf16[256,1024]{1,0:T(8,128)(2,1)}, u32[]{:S(2)}, u32[]{:S(2)}) collective-permute-start(bf16[256,1024]{1,0:T(8,128)(2,1)} %collective-permute-done.6), channel_id=1, source_target_pairs={{0,9},{1,10},{2,11},{3,12},{4,13},{5,14},{6,15},{7,8},{8,7},{9,0},... | collective-permute-start | bytes 1572872 | tf_op jit(solution)/shard_map/ppermute | solution.py:68
  60.7 13.1 %all-to-all-start.1 = ((bf16[8,8,2,128]{3,2,1,0:T(2,128)(2,1)}), bf16[8,8,2,128]{3,2,1,0:T(2,128)(2,1)S(1)}, u32[]{:S(2)}, u32[]{:S(2)}) async-start(bf16[8,8,2,128]{3,2,1,0:T(2,128)(2,1)} %broadcast_in_dim.13), calls=%async_computation.1 | async-start | bytes 65536 | tf_op jit(solution)/shard_map/all_to_all | solution.py:15
  64.1 22.2 %collective-permute-start.5 = (bf16[256,1024]{1,0:T(8,128)(2,1)}, bf16[256,1024]{1,0:T(8,128)(2,1)S(1)}, u32[]{:S(2)}, u32[]{:S(2)}) collective-permute-start(bf16[256,1024]{1,0:T(8,128)(2,1)} %collective-permute-done.4), channel_id=1, source_target_pairs={{0,8},{1,9},{2,10},{3,11},{4,12},{5,13},{6,14},{7,15},{8,0},{9,1},... | collective-permute-start | bytes 1572872 | tf_op jit(solution)/shard_map/ppermute | solution.py:68
  67.1 19.2 %collective-permute-start.7 = (bf16[256,1024]{1,0:T(8,128)(2,1)}, bf16[256,1024]{1,0:T(8,128)(2,1)S(1)}, u32[]{:S(2)}, u32[]{:S(2)}) collective-permute-start(bf16[256,1024]{1,0:T(8,128)(2,1)} %collective-permute-done.6), channel_id=1, source_target_pairs={{0,8},{1,9},{2,10},{3,11},{4,12},{5,13},{6,14},{7,15},{8,0},{9,1},... | collective-permute-start | bytes 1572872 | tf_op jit(solution)/shard_map/ppermute | solution.py:68
  69.0 18.3 %collective-permute-start.3 = (bf16[256,1024]{1,0:T(8,128)(2,1)S(1)}, bf16[256,1024]{1,0:T(8,128)(2,1)}, u32[]{:S(2)}, u32[]{:S(2)}) collective-permute-start(bf16[256,1024]{1,0:T(8,128)(2,1)S(1)} %collective-permute-done.2.refs_2_), channel_id=1, source_target_pairs={{0,1},{1,2},{2,3},{3,4},{4,5},{5,6},{6,7},{7,0},{8,15},{9,8},{10,9... | collective-permute-start | bytes 1572872 | tf_op jit(solution)/shard_map/ppermute | solution.py:68
  74.6 10.9 %all-to-all-start.2 = ((bf16[8,8,16,128]{3,2,1,0:T(8,128)(2,1)}), bf16[8,8,16,128]{3,2,1,0:T(8,128)(2,1)S(1)}, u32[]{:S(2)}, u32[]{:S(2)}) async-start(bf16[8,8,16,128]{3,2,1,0:T(8,128)(2,1)} %broadcast_in_dim.14), calls=%async_computation.2 | async-start | bytes 524288 | tf_op jit(solution)/shard_map/all_to_all | solution.py:15

commit v2 on v1

--- a/solution.py
+++ b/solution.py
@@ -23,7 +23,7 @@
         out_ref, sems = refs[-2:]
         n = lax.axis_size("rows")
         rows = out_ref.shape[0] // n
-        z, way = lax.axis_index("rows"), 1 - 2 * lax.axis_index("core")
+        z, way = lax.axis_index("rows"), 2 * lax.axis_index("core") - 1
         copies = []
         for i, (which, part, turn) in enumerate(pieces):
             at = pl.multiple_of(((z + turn * way + n) % n) * rows, rows)
@@ -47,6 +47,34 @@
     )(*arrays, *([] if fresh else [out]))
 
 
+def turned(shard, pieces=4):
+    inner, rows = shard.shape
+    step = inner // pieces
+
+    def body(shard_ref, out_ref, buf, sems):
+        copies = [
+            pltpu.make_async_copy(shard_ref.at[pl.ds(i * step, step)], buf.at[i], sems.at[i])
+            for i in range(pieces)
+        ]
+        for copy in copies:
+            copy.start()
+        for i in range(pieces):
+            copies[i].wait()
+            out_ref[:, i * step : (i + 1) * step] = jnp.transpose(buf[i].astype(jnp.bfloat16))
+
+    return pl.pallas_call(
+        body,
+        out_shape=jax.ShapeDtypeStruct((rows, inner), jnp.bfloat16),
+        in_specs=[pl.BlockSpec(memory_space=pltpu.HBM)],
+        out_specs=pl.BlockSpec(memory_space=pltpu.VMEM),
+        scratch_shapes=[
+            pltpu.VMEM((pieces, step, rows), jnp.float32),
+            pltpu.SemaphoreType.DMA((pieces,)),
+        ],
+        compiler_params=pltpu.CompilerParams(vmem_limit_bytes=8 << 20),
+    )(pltpu.with_memory_space_constraint(shard, pltpu.HBM))
+
+
 def on_device(train_down, router_weight, router_gain):
     n, g = lax.axis_size("rows"), lax.axis_size(OWNER)
     ax = (*OWNER, "rows")
@@ -55,7 +83,7 @@
         out = []
         for a in range(g):
             for i in range(n):
-                way = 1 if (a + core) % 2 == 0 else -1
+                way = -1 if (a + core) % 2 == 0 else 1
                 out.append((a * n + i, (a ^ turn) * n + (i + way) % n))
         return out
 
@@ -67,7 +95,7 @@
     def send(x, perm):
         return lax.ppermute(x, ax, perm)
 
-    block = jnp.transpose(train_down[0]).astype(jnp.bfloat16)
+    block = pltpu.with_memory_space_constraint(turned(train_down[0]), pltpu.VMEM)
     rows, width = block.shape
 
     o1 = send(block, along)

time: 89.8 us -> 91 us (1.013)
  waiting for transfers between devices: 14.2 us -> 20.2 us
  starting transfers between devices: 50.6 us -> 45.9 us
  local copies, waits for them, and re-layouts: 3.61 us -> 2.18 us
  Pallas kernels: 6.02 us -> 7.37 us
    ppermute x9, starting transfers between devices: 42.8 us -> 32.1 us  [send(): return lax.ppermute(x, ax, perm)]
    all_to_all x2, starting transfers between devices: 7.75 us -> 13.9 us  [a2a(): return lax.all_to_all(copies, axis, split_axis=0, concat_axis=0, tiled=True)]
    ppermute x9, waiting for transfers between devices: 11 us -> 16.9 us  [send(): return lax.ppermute(x, ax, perm)]
    unnamed x3 -> x2, local copies, waits for them, and re-layouts: 2.22 us -> 0.79 us
    pallas_call x0 -> x1, Pallas kernels: none -> 1.35 us  [turned(): pl.pallas_call(body, out_shape=jax.ShapeDtypeStruct((rows, inner), jnp.bf...]
  transfers between devices with their start and end apart: 11 -> 11, of which waited for: 4 -> 5; matrix products, arithmetic and copies ran while one was open for 3% -> 3% of each run, Pallas kernels for 5% -> 5%
where the time goes in v2:
time: 91 us; the launch traced here: 90.3 us
  starting transfers between devices  45.9 us (50%)
  waiting for transfers between devices  20.2 us (22%)
  blocking collectives  13.2 us (15%)
  Pallas kernels  7.37 us (8%)
  local copies, waits for them, and re-layouts  2.18 us (2%)
    ppermute x9, starting transfers between devices, send(): return lax.ppermute(x, ax, perm)  32.1 us
    ppermute x9, waiting for transfers between devices, send(): return lax.ppermute(x, ax, perm)  16.9 us
    all_to_all x2, starting transfers between devices, a2a(): return lax.all_to_all(copies, axis, split_axis=0, concat_axis=0, tiled=True)  13.9 us
    all_to_all x1, blocking collectives, a2a(): return lax.all_to_all(copies, axis, split_axis=0, concat_axis=0, tiled=True)  13.2 us
    pallas_call x4, Pallas kernels, put(): pl.pallas_call(body, out_shape=jax.ShapeDtypeStruct(shape if fresh else o...  6.02 us
    all_to_all x2, waiting for transfers between devices, a2a(): return lax.all_to_all(copies, axis, split_axis=0, concat_axis=0, tiled=True)  3.26 us
  transfers between devices with their start and end apart: 11, of which 5 were waited for; matrix products, arithmetic and copies ran while one was open for 3% of the time, Pallas kernels for 5%

profile of v2, /device:TPU:1, one launch (start us, length us, event | category | flops | bytes accessed | tf_op | source)
XLA Modules:
  0.0 90.3 jit_solution(2819955091313433688)
XLA Ops:
  0.6 1.4 %shard_map.50.refs_0_ = bf16[256,1024]{1,0:T(8,128)(2,1)S(1)} custom-call(f32[1024,256]{1,0:T(8,128)} %bitcast.21), custom_call_target="tpu_custom_call" | custom-call | tf_op jit(solution)/shard_map/pallas_call | solution.py:65
  2.0 4.8 %collective-permute-start = (bf16[256,1024]{1,0:T(8,128)(2,1)S(1)}, bf16[256,1024]{1,0:T(8,128)(2,1)S(1)}, u32[]{:S(2)}, u32[]{:S(2)}) collective-permute-start(bf16[256,1024]{1,0:T(8,128)(2,1)S(1)} %shard_map.50.refs_0_), channel_id=1, source_target_pairs={{0,7},{1,0},{2,1},{3,2},{4,3},{5,4},{6,5},{7,6},{8,9},{9,10},{10,1... | collective-permute-start | bytes 1572872 | tf_op jit(solution)/shard_map/ppermute | solution.py:96
  6.8 9.7 %collective-permute-start.4 = (bf16[256,1024]{1,0:T(8,128)(2,1)S(1)}, bf16[256,1024]{1,0:T(8,128)(2,1)}, u32[]{:S(2)}, u32[]{:S(2)}) collective-permute-start(bf16[256,1024]{1,0:T(8,128)(2,1)S(1)} %shard_map.50.refs_0_), channel_id=1, source_target_pairs={{0,9},{1,10},{2,11},{3,12},{4,13},{5,14},{6,15},{7,8},{8,7},{9,0},... | collective-permute-start | bytes 1572872 | tf_op jit(solution)/shard_map/ppermute | solution.py:96
  16.5 5.8 %collective-permute-done.refs_0_ = bf16[256,1024]{1,0:T(8,128)(2,1)S(1)} collective-permute-done((bf16[256,1024]{1,0:T(8,128)(2,1)S(1)}, bf16[256,1024]{1,0:T(8,128)(2,1)S(1)}, u32[]{:S(2)}, u32[]{:S(2)}) %collective-permute-start) | collective-permute-done | bytes 524320 | tf_op jit(solution)/shard_map/ppermute | solution.py:96
  22.3 1.9 %collective-permute-start.1 = (bf16[256,1024]{1,0:T(8,128)(2,1)S(1)}, bf16[256,1024]{1,0:T(8,128)(2,1)S(1)}, u32[]{:S(2)}, u32[]{:S(2)}) collective-permute-start(bf16[256,1024]{1,0:T(8,128)(2,1)S(1)} %collective-permute-done.refs_0_), channel_id=1, source_target_pairs={{0,7},{1,0},{2,1},{3,2},{4,3},{5,4},{6,5},{7,6},{8,9},{9,10},{10,1... | collective-permute-start | bytes 1572872 | tf_op jit(solution)/shard_map/ppermute | solution.py:96
  24.2 2.1 %collective-permute-done.4 = bf16[256,1024]{1,0:T(8,128)(2,1)} collective-permute-done((bf16[256,1024]{1,0:T(8,128)(2,1)S(1)}, bf16[256,1024]{1,0:T(8,128)(2,1)}, u32[]{:S(2)}, u32[]{:S(2)}) %collective-permute-start.4) | collective-permute-done | bytes 524320 | tf_op jit(solution)/shard_map/ppermute | solution.py:96
  26.3 1.9 %collective-permute-start.6 = (bf16[256,1024]{1,0:T(8,128)(2,1)}, bf16[256,1024]{1,0:T(8,128)(2,1)}, u32[]{:S(2)}, u32[]{:S(2)}) collective-permute-start(bf16[256,1024]{1,0:T(8,128)(2,1)} %collective-permute-done.4), channel_id=1, source_target_pairs={{0,7},{1,0},{2,1},{3,2},{4,3},{5,4},{6,5},{7,6},{8,9},{9,10},{10,1... | collective-permute-start | bytes 1572872 | tf_op jit(solution)/shard_map/ppermute | solution.py:96
  28.3 5.2 %collective-permute-done.1.refs_1_ = bf16[256,1024]{1,0:T(8,128)(2,1)S(1)} collective-permute-done((bf16[256,1024]{1,0:T(8,128)(2,1)S(1)}, bf16[256,1024]{1,0:T(8,128)(2,1)S(1)}, u32[]{:S(2)}, u32[]{:S(2)}) %collective-permute-start.1) | collective-permute-done | bytes 524320 | tf_op jit(solution)/shard_map/ppermute | solution.py:96
  33.5 1.9 %collective-permute-start.2 = (bf16[256,1024]{1,0:T(8,128)(2,1)S(1)}, bf16[256,1024]{1,0:T(8,128)(2,1)S(1)}, u32[]{:S(2)}, u32[]{:S(2)}) collective-permute-start(bf16[256,1024]{1,0:T(8,128)(2,1)S(1)} %collective-permute-done.1.refs_1_), channel_id=1, source_target_pairs={{0,7},{1,0},{2,1},{3,2},{4,3},{5,4},{6,5},{7,6},{8,9},{9,10},{10,1... | collective-permute-start | bytes 1572872 | tf_op jit(solution)/shard_map/ppermute | solution.py:96
  35.4 3.8 %collective-permute-done.6 = bf16[256,1024]{1,0:T(8,128)(2,1)} collective-permute-done((bf16[256,1024]{1,0:T(8,128)(2,1)}, bf16[256,1024]{1,0:T(8,128)(2,1)}, u32[]{:S(2)}, u32[]{:S(2)}) %collective-permute-start.6) | collective-permute-done | bytes 524320 | tf_op jit(solution)/shard_map/ppermute | solution.py:96
  39.2 3.7 %collective-permute-start.8 = (bf16[256,1024]{1,0:T(8,128)(2,1)}, bf16[256,1024]{1,0:T(8,128)(2,1)}, u32[]{:S(2)}, u32[]{:S(2)}) collective-permute-start(bf16[256,1024]{1,0:T(8,128)(2,1)} %collective-permute-done.6), channel_id=1, source_target_pairs={{0,15},{1,8},{2,9},{3,10},{4,11},{5,12},{6,13},{7,14},{8,1},{9,2},... | collective-permute-start | bytes 1572872 | tf_op jit(solution)/shard_map/ppermute | solution.py:96
  42.9 0.7 fusion
  43.6 13.2 %all_to_all.15 = bf16[8,2,128]{2,1,0:T(2,128)(2,1)S(1)} all-to-all(bf16[8,2,128]{2,1,0:T(2,128)(2,1)S(1)} %broadcast_in_dim.12), channel_id=1, replica_groups=mesh['y'=8,'x'=4,'core'=2,'rows'=8] {'y'}, dimensions={0} | all-to-all | bytes 8192 | tf_op jit(solution)/shard_map/all_to_all | solution.py:15
  56.8 0.6 broadcast_in_dim.13
  57.4 7.6 %all-to-all-start.1 = ((bf16[8,8,2,128]{3,2,1,0:T(2,128)(2,1)}), bf16[8,8,2,128]{3,2,1,0:T(2,128)(2,1)S(1)}, u32[]{:S(2)}, u32[]{:S(2)}) async-start(bf16[8,8,2,128]{3,2,1,0:T(2,128)(2,1)} %broadcast_in_dim.13), calls=%async_computation.1 | async-start | bytes 65536 | tf_op jit(solution)/shard_map/all_to_all | solution.py:15
  65.0 2.5 %collective-permute-start.5 = (bf16[256,1024]{1,0:T(8,128)(2,1)}, bf16[256,1024]{1,0:T(8,128)(2,1)S(1)}, u32[]{:S(2)}, u32[]{:S(2)}) collective-permute-start(bf16[256,1024]{1,0:T(8,128)(2,1)} %collective-permute-done.4), channel_id=1, source_target_pairs={{0,8},{1,9},{2,10},{3,11},{4,12},{5,13},{6,14},{7,15},{8,0},{9,1},... | collective-permute-start | bytes 1572872 | tf_op jit(solution)/shard_map/ppermute | solution.py:96
  67.6 1.9 %collective-permute-start.7 = (bf16[256,1024]{1,0:T(8,128)(2,1)}, bf16[256,1024]{1,0:T(8,128)(2,1)S(1)}, u32[]{:S(2)}, u32[]{:S(2)}) collective-permute-start(bf16[256,1024]{1,0:T(8,128)(2,1)} %collective-permute-done.6), channel_id=1, source_target_pairs={{0,8},{1,9},{2,10},{3,11},{4,12},{5,13},{6,14},{7,15},{8,0},{9,1},... | collective-permute-start | bytes 1572872 | tf_op jit(solution)/shard_map/ppermute | solution.py:96
  69.5 0.0 collective-permute-done.2.refs_2_
  69.5 3.7 %collective-permute-start.3 = (bf16[256,1024]{1,0:T(8,128)(2,1)S(1)}, bf16[256,1024]{1,0:T(8,128)(2,1)}, u32[]{:S(2)}, u32[]{:S(2)}) collective-permute-start(bf16[256,1024]{1,0:T(8,128)(2,1)S(1)} %collective-permute-done.2.refs_2_), channel_id=1, source_target_pairs={{0,7},{1,0},{2,1},{3,2},{4,3},{5,4},{6,5},{7,6},{8,9},{9,10},{10,1... | collective-permute-start | bytes 1572872 | tf_op jit(solution)/shard_map/ppermute | solution.py:96
  73.2 0.0 all-to-all-done.1
  73.2 0.7 broadcast_in_dim.14
  73.9 6.3 %all-to-all-start.2 = ((bf16[8,8,16,128]{3,2,1,0:T(8,128)(2,1)}), bf16[8,8,16,128]{3,2,1,0:T(8,128)(2,1)S(1)}, u32[]{:S(2)}, u32[]{:S(2)}) async-start(bf16[8,8,16,128]{3,2,1,0:T(8,128)(2,1)} %broadcast_in_dim.14), calls=%async_computation.2 | async-start | bytes 524288 | tf_op jit(solution)/shard_map/all_to_all | solution.py:15
  80.2 0.8 shard_map.51.refs_4_
  81.0 0.0 collective-permute-done.8.refs_3_
  81.0 2.4 %shard_map.52.refs_2_ = bf16[2048,1024]{1,0:T(8,128)(2,1)} custom-call(bf16[256,1024]{1,0:T(8,128)(2,1)S(1)} %collective-permute-done.refs_0_, bf16[256,1024]{1,0:T(8,128)(2,1)S(1)} %collective-permute-done.1.refs_1_, bf16[256,1024]{1,0:T(8,128)(2,1)S(1)} %collective-permute-done.2.refs_2_, ...), custom_call_target="tpu_custom_call", output_to_operand_aliasing={{}: (4, {})} | custom-call | tf_op jit(solution)/shard_map/pallas_call | solution.py:39
  83.4 3.3 %all-to-all-done.2 = bf16[8,8,16,128]{3,2,1,0:T(8,128)(2,1)S(1)} async-done(((bf16[8,8,16,128]{3,2,1,0:T(8,128)(2,1)}), bf16[8,8,16,128]{3,2,1,0:T(8,128)(2,1)S(1)}, u32[]{:S(2)}, u32[]{:S(2)}) %all-to-all-start.2) | async-done | bytes 262176 | tf_op jit(solution)/shard_map/all_to_all | solution.py:15
  86.7 0.8 copy.14
  87.5 0.0 collective-permute-done.5.refs_0_
  87.5 0.0 collective-permute-done.7.refs_1_
  87.5 1.0 %shard_map.53.refs_1_ = bf16[2048,1024]{1,0:T(8,128)(2,1)} custom-call(bf16[256,1024]{1,0:T(8,128)(2,1)S(1)} %collective-permute-done.5.refs_0_, bf16[256,1024]{1,0:T(8,128)(2,1)S(1)} %collective-permute-done.7.refs_1_, bf16[2048,1024]{1,0:T(8,128)(2,1)} %shard_map.52.refs_2_), custom_call_target="tpu_custom_call", output_to_operand_aliasing={{}: (2, {})} | custom-call | tf_op jit(solution)/shard_map/pallas_call | solution.py:39
  88.5 0.0 collective-permute-done.3.refs_0_
  88.5 1.8 %shard_map.54 = bf16[2048,1024]{1,0:T(8,128)(2,1)} custom-call(bf16[256,1024]{1,0:T(8,128)(2,1)} %collective-permute-done.3.refs_0_, bf16[2048,1024]{1,0:T(8,128)(2,1)} %shard_map.53.refs_1_), custom_call_target="tpu_custom_call", output_to_operand_aliasing={{}: (1, {})} | custom-call | tf_op jit(solution)/shard_map/pallas_call | solution.py:39
  (4 shorter events, 0.0 us)
Async XLA Ops:
  2.0 20.3 %collective-permute-start = (bf16[256,1024]{1,0:T(8,128)(2,1)S(1)}, bf16[256,1024]{1,0:T(8,128)(2,1)S(1)}, u32[]{:S(2)}, u32[]{:S(2)}) collective-permute-start(bf16[256,1024]{1,0:T(8,128)(2,1)S(1)} %shard_map.50.refs_0_), channel_id=1, source_target_pairs={{0,7},{1,0},{2,1},{3,2},{4,3},{5,4},{6,5},{7,6},{8,9},{9,10},{10,1... | collective-permute-start | bytes 1572872 | tf_op jit(solution)/shard_map/ppermute | solution.py:96
  6.8 19.5 %collective-permute-start.4 = (bf16[256,1024]{1,0:T(8,128)(2,1)S(1)}, bf16[256,1024]{1,0:T(8,128)(2,1)}, u32[]{:S(2)}, u32[]{:S(2)}) collective-permute-start(bf16[256,1024]{1,0:T(8,128)(2,1)S(1)} %shard_map.50.refs_0_), channel_id=1, source_target_pairs={{0,9},{1,10},{2,11},{3,12},{4,13},{5,14},{6,15},{7,8},{8,7},{9,0},... | collective-permute-start | bytes 1572872 | tf_op jit(solution)/shard_map/ppermute | solution.py:96
  22.3 11.1 %collective-permute-start.1 = (bf16[256,1024]{1,0:T(8,128)(2,1)S(1)}, bf16[256,1024]{1,0:T(8,128)(2,1)S(1)}, u32[]{:S(2)}, u32[]{:S(2)}) collective-permute-start(bf16[256,1024]{1,0:T(8,128)(2,1)S(1)} %collective-permute-done.refs_0_), channel_id=1, source_target_pairs={{0,7},{1,0},{2,1},{3,2},{4,3},{5,4},{6,5},{7,6},{8,9},{9,10},{10,1... | collective-permute-start | bytes 1572872 | tf_op jit(solution)/shard_map/ppermute | solution.py:96
  26.3 12.8 %collective-permute-start.6 = (bf16[256,1024]{1,0:T(8,128)(2,1)}, bf16[256,1024]{1,0:T(8,128)(2,1)}, u32[]{:S(2)}, u32[]{:S(2)}) collective-permute-start(bf16[256,1024]{1,0:T(8,128)(2,1)} %collective-permute-done.4), channel_id=1, source_target_pairs={{0,7},{1,0},{2,1},{3,2},{4,3},{5,4},{6,5},{7,6},{8,9},{9,10},{10,1... | collective-permute-start | bytes 1572872 | tf_op jit(solution)/shard_map/ppermute | solution.py:96
  33.5 36.0 %collective-permute-start.2 = (bf16[256,1024]{1,0:T(8,128)(2,1)S(1)}, bf16[256,1024]{1,0:T(8,128)(2,1)S(1)}, u32[]{:S(2)}, u32[]{:S(2)}) collective-permute-start(bf16[256,1024]{1,0:T(8,128)(2,1)S(1)} %collective-permute-done.1.refs_1_), channel_id=1, source_target_pairs={{0,7},{1,0},{2,1},{3,2},{4,3},{5,4},{6,5},{7,6},{8,9},{9,10},{10,1... | collective-permute-start | bytes 1572872 | tf_op jit(solution)/shard_map/ppermute | solution.py:96
  39.2 41.8 %collective-permute-start.8 = (bf16[256,1024]{1,0:T(8,128)(2,1)}, bf16[256,1024]{1,0:T(8,128)(2,1)}, u32[]{:S(2)}, u32[]{:S(2)}) collective-permute-start(bf16[256,1024]{1,0:T(8,128)(2,1)} %collective-permute-done.6), channel_id=1, source_target_pairs={{0,15},{1,8},{2,9},{3,10},{4,11},{5,12},{6,13},{7,14},{8,1},{9,2},... | collective-permute-start | bytes 1572872 | tf_op jit(solution)/shard_map/ppermute | solution.py:96
  57.4 15.8 %all-to-all-start.1 = ((bf16[8,8,2,128]{3,2,1,0:T(2,128)(2,1)}), bf16[8,8,2,128]{3,2,1,0:T(2,128)(2,1)S(1)}, u32[]{:S(2)}, u32[]{:S(2)}) async-start(bf16[8,8,2,128]{3,2,1,0:T(2,128)(2,1)} %broadcast_in_dim.13), calls=%async_computation.1 | async-start | bytes 65536 | tf_op jit(solution)/shard_map/all_to_all | solution.py:15
  65.0 22.5 %collective-permute-start.5 = (bf16[256,1024]{1,0:T(8,128)(2,1)}, bf16[256,1024]{1,0:T(8,128)(2,1)S(1)}, u32[]{:S(2)}, u32[]{:S(2)}) collective-permute-start(bf16[256,1024]{1,0:T(8,128)(2,1)} %collective-permute-done.4), channel_id=1, source_target_pairs={{0,8},{1,9},{2,10},{3,11},{4,12},{5,13},{6,14},{7,15},{8,0},{9,1},... | collective-permute-start | bytes 1572872 | tf_op jit(solution)/shard_map/ppermute | solution.py:96
  67.6 19.9 %collective-permute-start.7 = (bf16[256,1024]{1,0:T(8,128)(2,1)}, bf16[256,1024]{1,0:T(8,128)(2,1)S(1)}, u32[]{:S(2)}, u32[]{:S(2)}) collective-permute-start(bf16[256,1024]{1,0:T(8,128)(2,1)} %collective-permute-done.6), channel_id=1, source_target_pairs={{0,8},{1,9},{2,10},{3,11},{4,12},{5,13},{6,14},{7,15},{8,0},{9,1},... | collective-permute-start | bytes 1572872 | tf_op jit(solution)/shard_map/ppermute | solution.py:96
  69.5 19.0 %collective-permute-start.3 = (bf16[256,1024]{1,0:T(8,128)(2,1)S(1)}, bf16[256,1024]{1,0:T(8,128)(2,1)}, u32[]{:S(2)}, u32[]{:S(2)}) collective-permute-start(bf16[256,1024]{1,0:T(8,128)(2,1)S(1)} %collective-permute-done.2.refs_2_), channel_id=1, source_target_pairs={{0,7},{1,0},{2,1},{3,2},{4,3},{5,4},{6,5},{7,6},{8,9},{9,10},{10,1... | collective-permute-start | bytes 1572872 | tf_op jit(solution)/shard_map/ppermute | solution.py:96
  73.9 12.8 %all-to-all-start.2 = ((bf16[8,8,16,128]{3,2,1,0:T(8,128)(2,1)}), bf16[8,8,16,128]{3,2,1,0:T(8,128)(2,1)S(1)}, u32[]{:S(2)}, u32[]{:S(2)}) async-start(bf16[8,8,16,128]{3,2,1,0:T(8,128)(2,1)} %broadcast_in_dim.14), calls=%async_computation.2 | async-start | bytes 524288 | tf_op jit(solution)/shard_map/all_to_all | solution.py:15
